TPU v7x, 16 devices: a 4x2x1 block of a 4x4x8 slice. The times are simulated.
16 devices in a mesh: rep: 2 (over y, z), dp: 8 (over x, core).
Axes of the slice: x: 4, y: 2, z: 1, core: 2. Of those that a mesh axis runs over, the one named last changes fastest.
The devices are a block of a 4x4x8 slice.
Arguments:
- hidden: bfloat16 [1024, 2560], P(('rep', 'dp')), parts along dimension 0
- ckv_cache: bfloat16 [1024, 1024, 256], P(('rep', 'dp')), parts along dimension 0
- kpe_cache: bfloat16 [1024, 1024, 32], P(('rep', 'dp')), parts along dimension 0
- cache_len: int32 [1024], P(('rep', 'dp')), parts along dimension 0
- rope_cos: float32 [1024, 16], P(('rep', 'dp')), parts along dimension 0
- rope_sin: float32 [1024, 16], P(('rep', 'dp')), parts along dimension 0
- norm_attn: float32 [2560], replicated
- w_dq: bfloat16 [2560, 768], replicated
- norm_q: float32 [768], replicated
- w_uq: bfloat16 [768, 40, 96], replicated
- w_dkv: bfloat16 [2560, 288], replicated
- norm_kv: float32 [256], replicated
- w_uk: bfloat16 [256, 40, 64], replicated
- w_uv: bfloat16 [256, 40, 64], replicated
- w_out: bfloat16 [40, 64, 2560], replicated
- norm_mlp: float32 [2560], replicated
- w_gate: bfloat16 [2560, 6400], P(None, 'dp')
- w_up: bfloat16 [2560, 6400], P(None, 'dp')
- w_down: bfloat16 [6400, 2560], P('dp')
Outputs:
- output 1: bfloat16 [1024, 2560], P(('rep', 'dp')), parts along dimension 0
- output 2: bfloat16 [1024, 256], P(('rep', 'dp')), parts along dimension 0
- output 3: bfloat16 [1024, 32], P(('rep', 'dp')), parts along dimension 0
There are 2 independent parts. A program takes and returns all parts, laid end to end along the dimension named above; an argument that names none is the same for every part.
All inputs are finite; a program needn't handle non-finite values.
Results may differ from a plain program's by a relative error of at most 0.010691.
Values are sent between devices in bfloat16 or wider.
A program may use at most 768 MiB of HBM per device.

v0:
```python
import math
import jax
import jax.numpy as jnp
from jax import lax
from jax.sharding import PartitionSpec as P

EPSILON = 1e-6
MSCALE = 0.1 * math.log(40.0) + 1.0


def rms_norm(values_in, gain_vec):
    floats = values_in.astype(jnp.float32)
    mean_sq = jnp.mean(floats * floats, axis=-1, keepdims=True)
    return floats * lax.rsqrt(mean_sq + EPSILON) * gain_vec


def apply_rope(values_in, cos_t, sin_t):
    half_dim = values_in.shape[-1] // 2
    low_half = values_in[..., :half_dim]
    high_half = values_in[..., half_dim:]
    return jnp.concatenate([low_half * cos_t - high_half * sin_t, high_half * cos_t + low_half * sin_t], axis=-1)


def attention_rows(hidden, ckv_cache, kpe_cache, cache_len, rope_cos, rope_sin, norm_attn, w_dq, norm_q, w_uq, w_dkv, norm_kv, w_uk, w_uv, w_out):
    nope_dim = w_uk.shape[2]
    value_a7 = w_uk.shape[0]
    score_scale = MSCALE * MSCALE / math.sqrt(w_uq.shape[2])
    normed = rms_norm(hidden, norm_attn).astype(jnp.bfloat16)
    q_latent = rms_norm(jnp.dot(normed, w_dq, preferred_element_type=jnp.float32), norm_q).astype(jnp.bfloat16)
    q_full = jnp.einsum('bl,lhe->bhe', q_latent, w_uq, preferred_element_type=jnp.float32)
    q_nope = q_full[..., :nope_dim].astype(jnp.bfloat16)
    q_pe = apply_rope(q_full[..., nope_dim:], rope_cos[:, None, :], rope_sin[:, None, :]).astype(jnp.bfloat16)
    kv_full = jnp.dot(normed, w_dkv, preferred_element_type=jnp.float32)
    ckv_new = rms_norm(kv_full[:, :value_a7], norm_kv).astype(jnp.bfloat16)
    kpe_new = apply_rope(kv_full[:, value_a7:], rope_cos, rope_sin).astype(jnp.bfloat16)
    q_abs = jnp.einsum('bhn,lhn->bhl', q_nope, w_uk, preferred_element_type=jnp.float32).astype(jnp.bfloat16)
    scores = (jnp.einsum('bhl,btl->bht', q_abs, ckv_cache, preferred_element_type=jnp.float32)
              + jnp.einsum('bhr,btr->bht', q_pe, kpe_cache, preferred_element_type=jnp.float32)) * score_scale
    positions = jnp.arange(ckv_cache.shape[1])
    scores = jnp.where(positions[None, None, :] < cache_len[:, None, None], scores, -jnp.inf)
    score_new = (jnp.einsum('bhl,bl->bh', q_abs, ckv_new, preferred_element_type=jnp.float32)
                 + jnp.einsum('bhr,br->bh', q_pe, kpe_new, preferred_element_type=jnp.float32)) * score_scale
    row_max = jnp.maximum(jnp.max(scores, axis=-1), score_new)
    exp_cache = jnp.exp(scores - row_max[..., None])
    exp_new = jnp.exp(score_new - row_max)
    norm_sum = jnp.sum(exp_cache, axis=-1) + exp_new
    weighted = (jnp.einsum('bht,btl->bhl', exp_cache.astype(jnp.bfloat16), ckv_cache, preferred_element_type=jnp.float32)
                + exp_new.astype(jnp.bfloat16).astype(jnp.float32)[..., None] * ckv_new.astype(jnp.float32)[:, None, :])
    lat_out = (weighted / norm_sum[..., None]).astype(jnp.bfloat16)
    head_out = jnp.einsum('bhl,lhv->bhv', lat_out, w_uv, preferred_element_type=jnp.float32).astype(jnp.bfloat16)
    attn_out = jnp.einsum('bhv,hvd->bd', head_out, w_out, preferred_element_type=jnp.float32)
    residual = (hidden.astype(jnp.float32) + attn_out).astype(jnp.bfloat16)
    return residual, ckv_new, kpe_new


def solution(mesh):
    row_spec = P(('rep', 'dp'), None)
    cube_spec = P(('rep', 'dp'), None, None)
    full_spec = P()
    in_specs = (row_spec, cube_spec, cube_spec, P(('rep', 'dp')), row_spec, row_spec,
                full_spec, full_spec, full_spec, full_spec, full_spec, full_spec, full_spec, full_spec, full_spec, full_spec,
                P(None, 'dp'), P(None, 'dp'), P('dp', None))

    def local_step(hidden, ckv_cache, kpe_cache, cache_len, rope_cos, rope_sin, norm_attn, w_dq, norm_q, w_uq, w_dkv, norm_kv, w_uk, w_uv, w_out, norm_mlp, w_gate, w_up, w_down):
        residual, ckv_new, kpe_new = attention_rows(hidden, ckv_cache, kpe_cache, cache_len, rope_cos, rope_sin, norm_attn, w_dq, norm_q, w_uq, w_dkv, norm_kv, w_uk, w_uv, w_out)
        mlp_in = rms_norm(residual, norm_mlp).astype(jnp.bfloat16)
        group_in = lax.all_gather(mlp_in, 'dp', axis=0, tiled=True)
        gate_val = jnp.dot(group_in, w_gate, preferred_element_type=jnp.float32)
        up_val = jnp.dot(group_in, w_up, preferred_element_type=jnp.float32)
        act_val = (jax.nn.silu(gate_val) * up_val).astype(jnp.bfloat16)
        partial_sum = jnp.dot(act_val, w_down, preferred_element_type=jnp.float32)
        mlp_rows = lax.psum_scatter(partial_sum, 'dp', scatter_dimension=0, tiled=True)
        out_hidden = (residual.astype(jnp.float32) + mlp_rows).astype(jnp.bfloat16)
        return out_hidden, ckv_new, kpe_new

    return jax.shard_map(local_step, mesh=mesh, in_specs=in_specs, out_specs=(row_spec, row_spec, row_spec), check_vma=False)
```

profile of v0, /device:TPU:112, one launch (start us, length us, event | category | flops | bytes accessed | tf_op | source)
XLA Modules:
  0.0 177.7 jit_solution(2440979134539073723)
XLA Ops:
  7.2 0.0 copy-start
  7.2 0.0 copy-start.2
  7.2 0.0 copy-start.4
  7.2 0.0 copy-start.7
  7.2 0.0 copy-start.6
  7.2 0.1 all-gather.2.cloned.1.call-start
  7.3 1.2 fusion.24
  8.6 0.1 copy-done
  8.7 1.6 fusion.33
  10.3 0.0 copy-start.9
  10.3 0.1 multiply_reduce_fusion.2
  10.4 0.1 fusion.44
  10.5 0.8 copy.32
  11.3 0.8 copy.33
  12.0 0.8 iota_compare_fusion
  12.8 0.1 copy.43
  12.9 0.1 copy.42
  12.9 0.0 copy-done.7
  12.9 0.0 copy-done.6
  13.0 0.1 copy.39
  13.1 3.1 %multiply_reduce_fusion.1 = (f32[64]{0:T(128)S(1)}, f32[64,768]{1,0:T(8,128)S(1)}) fusion(bf16[2560,768]{1,0:T(8,128)(2,1)} %param.26, bf16[64,2560]{1,0:T(8,128)(2,1)S(1)} %copy-done.2, f32[2560]{0:T(1024)S(1)} %copy-done.4, f32[64]{0:T(128)S(1)} %add_rsqrt_fusion.3), kind=kOutput, calls=%fused_computation.39 | convolution fusion | flops 252411840 | bytes 4467200 | tf_op jit(solution)/shard_map/dot_general | solution.py:29
  16.2 0.0 copy-start.3
  16.2 5.0 %fusion.29 = f32[64,40,96]{2,0,1:T(8,128)S(1)} fusion(bf16[768,40,96]{0,2,1:T(8,128)(2,1)} %param.28, f32[64,768]{1,0:T(8,128)S(1)} %get-tuple-element.17, f32[768]{0:T(1024)S(1)} %copy-done.9, f32[64]{0:T(128)S(1)} %add_rsqrt_fusion.2), kind=kOutput, calls=%fused_computation.41 | convolution fusion | flops 377634816 | bytes 7081216 | tf_op jit(solution)/shard_map/bl,lhe->bhe/dot_general | solution.py:30
  21.3 0.0 copy-done.3
  21.3 0.5 fusion.13
  21.8 0.7 subtract_convert_fusion
  22.5 0.4 pad_maximum_fusion
  22.9 0.8 copy.34
  23.6 0.3 fusion.48
  23.9 7.7 %fusion.47 = f32[64,40,1024]{2,1,0:T(8,128)} fusion(bf16[64,40,32]{1,2,0:T(8,128)(2,1)S(1)} %copy.34, bf16[64,1024,32]{1,2,0:T(8,128)(2,1)} %param.21), kind=kOutput, calls=%fused_computation.66 | convolution fusion | flops 167772160 | bytes 14843904 | tf_op jit(solution)/shard_map/bhr,btr->bht/dot_general | solution.py:38
  31.6 0.1 fusion.43
  31.7 0.0 copy-start.5
  31.7 0.8 fusion.20
  32.6 20.4 %fusion.5 = (f32[64,40]{1,0:T(8,128)S(1)}, f32[64,40,1024]{2,1,0:T(8,128)}) fusion(f32[64,40,1024]{2,1,0:T(8,128)} %fusion.47, pred[64,1024]{1,0:T(8,128)(4,1)S(1)} %iota_compare_fusion, bf16[64,1024,256]{2,1,0:T(8,128)(2,1)} %param.20, bf16[64,40,256]{2,0,1:T(8,128)(2,1)S(1)} %fusion.13), kind=kOutput, calls=%fused_computation.6 | convolution fusion | flops 1352660480 | bytes 55912448 | tf_op jit(solution)/shard_map/bhl,btl->bht/dot_general | solution.py:37
  53.0 8.5 %fusion = f32[64,40]{1,0:T(8,128)S(1)} fusion(f32[64,40]{1,0:T(8,128)S(1)} %fusion.38, f32[64,40,1024]{2,1,0:T(8,128)} %get-tuple-element.19, f32[64,40,1024]{2,1,0:T(8,128)} %fusion.47, pred[64,1024]{1,0:T(8,128)(4,1)S(1)} %iota_compare_fusion), kind=kLoop, calls=%fused_computation.2 | loop fusion | flops 13104640 | bytes 21057536 | tf_op jit(solution)/shard_map/reduce_sum | solution.py:46
  61.5 19.6 %divide_convert_fusion = bf16[64,40,256]{2,1,0:T(8,128)(2,1)S(1)} fusion(bf16[64,1024,256]{2,1,0:T(8,128)(2,1)} %param.20, f32[64,40]{1,0:T(8,128)S(1)} %fusion.38, f32[64,40,1024]{2,1,0:T(8,128)} %get-tuple-element.19, f32[64,40,1024]{2,1,0:T(8,128)} %fusion.47, pred[64,1024]{1,0:T(8,128)(4,1)S(1)} %iota_compare_fusion, ...), kind=kOutput, calls=%fused_computation.13 | convolution fusion | flops 1357905920 | bytes 55998464 | tf_op jit(solution)/shard_map/bht,btl->bhl/dot_general | solution.py:47
  81.1 0.0 copy-start.8
  81.1 6.7 %multiply_reduce_fusion = (f32[64]{0:T(128)S(1)}, f32[64,2560]{1,0:T(8,128)S(1)}) fusion(bf16[40,64,2560]{2,1,0:T(8,128)(2,1)} %param.33, bf16[256,40,64]{0,2,1:T(8,128)(2,1)} %param.32, bf16[64,40,256]{2,1,0:T(8,128)(2,1)S(1)} %divide_convert_fusion, bf16[64,2560]{1,0:T(8,128)(2,1)S(1)} %copy-done.2), kind=kOutput, calls=%fused_computation.35 | convolution fusion | flops 923893696 | bytes 16711936 | tf_op jit(solution)/shard_map/bhv,hvd->bd/dot_general | solution.py:51
  87.8 0.9 multiply_convert_fusion.1
  88.6 0.1 all-gather.2.cloned.1.call-update
  88.7 0.3 reduce-scatter.2.cloned.1.call-start
  89.0 24.7 %all-gather.2.cloned.1.call-done = bf16[512,2560]{1,0:T(8,128)(2,1)} async-done(((bf16[64,2560]{1,0:T(8,128)(2,1)}), bf16[512,2560]{1,0:T(8,128)(2,1)}) %all-gather.2.cloned.1.call-update) | async-done | bytes 2621456 | tf_op jit(solution)/shard_map/all_gather | solution.py:67
  113.7 6.5 %fusion.49 = f32[512,800]{0,1:T(8,128)} fusion(bf16[512,2560]{1,0:T(8,128)(2,1)} %all-gather.2.cloned.1.call-done, bf16[2560,800]{0,1:T(8,128)(2,1)} %param.35), kind=kOutput, calls=%fused_computation.68 | convolution fusion | flops 2097152000 | bytes 8355840 | tf_op jit(solution)/shard_map/dot_general | solution.py:68
  120.2 12.1 %fusion.27 = f32[512,2560]{1,0:T(8,128)} fusion(bf16[800,2560]{1,0:T(8,128)(2,1)} %param.37, f32[512,800]{0,1:T(8,128)} %fusion.49, bf16[512,2560]{1,0:T(8,128)(2,1)} %all-gather.2.cloned.1.call-done, bf16[2560,800]{0,1:T(8,128)(2,1)} %param.36), kind=kOutput, calls=%fused_computation.36 | convolution fusion | flops 4196761600 | bytes 17694720 | tf_op jit(solution)/shard_map/dot_general | solution.py:71
  132.3 0.1 reduce-scatter.2.cloned.1.call-update
  132.4 0.6 pad_maximum_fusion.1
  133.0 36.0 %reduce-scatter.2.cloned.1.call-done = f32[64,2560]{1,0:T(8,128)} async-done(((f32[512,2560]{1,0:T(8,128)}), f32[64,2560]{1,0:T(8,128)}) %reduce-scatter.2.cloned.1.call-update) | async-done | bytes 655376 | tf_op jit(solution)/shard_map/reduce_scatter | solution.py:72
  169.0 1.9 %add_convert_fusion.1 = bf16[64,2560]{1,0:T(8,128)(2,1)} fusion(f32[64,2560]{1,0:T(8,128)S(1)} %get-tuple-element.21, f32[64,2560]{1,0:T(8,128)} %reduce-scatter.2.cloned.1.call-done), kind=kLoop, calls=%fused_computation.33 | loop fusion | flops 327680 | bytes 1638400 | tf_op jit(solution)/shard_map/convert_element_type | solution.py:73
  (17 shorter events, 0.1 us)
Async XLA Ops:
  7.2 1.5 copy-start
  7.2 5.9 %copy-start.2 = (bf16[64,2560]{1,0:T(8,128)(2,1)S(1)}, bf16[64,2560]{1,0:T(8,128)(2,1)}, u32[]{:S(2)}) copy-start(bf16[64,2560]{1,0:T(8,128)(2,1)} %param.19) | copy-start | bytes 983044
  7.2 5.9 %copy-start.4 = (f32[2560]{0:T(1024)S(1)}, f32[2560]{0:T(1024)}, u32[]{:S(2)}) copy-start(f32[2560]{0:T(1024)} %param.25) | copy-start | bytes 30724
  7.2 5.7 %copy-start.7 = (f32[64,16]{0,1:T(8,128)S(1)}, f32[64,16]{0,1:T(8,128)}, u32[]{:S(2)}) copy-start(f32[64,16]{0,1:T(8,128)} %param.23) | copy-start | bytes 12292
  7.2 5.7 %copy-start.6 = (f32[64,16]{0,1:T(8,128)S(1)}, f32[64,16]{0,1:T(8,128)}, u32[]{:S(2)}) copy-start(f32[64,16]{0,1:T(8,128)} %param.24) | copy-start | bytes 12292
  7.2 106.5 %all-gather.2.cloned.1.call-start = ((), (), s32[]{:S(2)}) async-start(), calls=%async_computation.1 | async-start | bytes 2949120 | tf_op jit(solution)/shard_map/all_gather | solution.py:67
  10.3 5.9 %copy-start.9 = (f32[768]{0:T(1024)S(1)}, f32[768]{0:T(1024)}, u32[]{:S(2)}) copy-start(f32[768]{0:T(1024)} %param.27) | copy-start | bytes 9220
  16.2 5.0 %copy-start.3 = (bf16[256,40,64]{0,2,1:T(8,128)(2,1)S(1)}, bf16[256,40,64]{0,2,1:T(8,128)(2,1)}, u32[]{:S(2)}) copy-start(bf16[256,40,64]{0,2,1:T(8,128)(2,1)} %param.31) | copy-start | bytes 3932164
  23.9 7.7 %copy-start.10 = (f32[256]{0:T(256)S(1)}, f32[256]{0:T(256)}, u32[]{:S(2)}) copy-start(f32[256]{0:T(256)} %param.30) | copy-start | bytes 3076
  31.7 21.3 %copy-start.5 = (bf16[64,256]{1,0:T(8,128)(2,1)}, bf16[64,256]{1,0:T(8,128)(2,1)S(1)}, u32[]{:S(2)}) copy-start(bf16[64,256]{1,0:T(8,128)(2,1)S(1)} %get-tuple-element.7) | copy-start | bytes 98308
  81.1 6.7 %copy-start.8 = (f32[2560]{0:T(1024)S(1)}, f32[2560]{0:T(1024)}, u32[]{:S(2)}) copy-start(f32[2560]{0:T(1024)} %param.34) | copy-start | bytes 30724
  88.7 80.3 %reduce-scatter.2.cloned.1.call-start = ((), (), s32[]{:S(2)}) async-start(), calls=%async_computation.2 | async-start | bytes 5898240 | tf_op jit(solution)/shard_map/reduce_scatter | solution.py:72
  132.3 38.6 %copy-start.1 = (bf16[2560,288]{0,1:T(8,128)(2,1)S(1)}, bf16[2560,288]{0,1:T(8,128)(2,1)}, u32[]{:S(2)}) copy-start(bf16[2560,288]{0,1:T(8,128)(2,1)} %param.29) | copy-start | bytes 4423684
Sparse Core Ops, SparseCore 0:
  88.8 24.8 all-gather.1
  132.5 36.4 reduce-scatter.1
where the time goes:
time: 178 us
  matrix products  84.2 us (47%)
  waiting for transfers between devices  60.8 us (34%)
  other arithmetic  15.2 us (9%)
  between operations  14.3 us (8%)
  local copies, waits for them, and re-layouts  2.81 us (2%)
    reduce_scatter x1, waiting for transfers between devices, local_step(): lax.psum_scatter(partial_sum, 'dp', scatter_dimension=0, tiled=True)  36 us
    all_gather x1, waiting for transfers between devices, local_step(): group_in = lax.all_gather(mlp_in, 'dp', axis=0, tiled=True)  24.7 us
    dot_general x1, matrix products, attention_rows(): jnp.einsum('bhl,btl->bht', q_abs, ckv_cache, preferred_element_type=jnp.f...  20.4 us
    dot_general x1, matrix products, attention_rows(): jnp.einsum('bht,btl->bhl', exp_cache.astype(jnp.bfloat16), ckv_cache, pre...  19.6 us
    dot_general x1, matrix products, local_step(): partial_sum = jnp.dot(act_val, w_down, preferred_element_type=jnp.float32)  12.1 us
    reduce_sum x1, other arithmetic, attention_rows(): norm_sum = jnp.sum(exp_cache, axis=-1) + exp_new  8.47 us
    dot_general x1, matrix products, attention_rows(): jnp.einsum('bhr,btr->bht', q_pe, kpe_cache, preferred_element_type=jnp.fl...  7.74 us
    dot_general x1, matrix products, attention_rows(): jnp.einsum('bhv,hvd->bd', head_out, w_out, preferred_element_type=jnp.flo...  6.66 us
  transfers between devices with their start and end apart: 2, of which 2 were waited for; matrix products, arithmetic and copies ran while one was open for 0% of the time, Pallas kernels for 0%

commit v1 on v0

v1 whole, which is shorter than its diff:
```python
import functools
import math

import jax
import jax.numpy as jnp
from jax import lax
from jax.experimental import pallas as pl
from jax.experimental.pallas import tpu as pltpu
from jax.sharding import PartitionSpec as P

EPSILON = 1e-6
MSCALE = 0.1 * math.log(40.0) + 1.0
F32 = jnp.float32
BF16 = jnp.bfloat16
NT = (((1,), (1,)), ((), ()))
VMEM_LIMIT = 64 * 1024 * 1024 - 65536


def dot(a, b):
    return jnp.dot(a, b, preferred_element_type=F32)


def dot_nt(a, b):
    return lax.dot_general(a, b, NT, preferred_element_type=F32)


def normed(v, gain):
    return v * lax.rsqrt(jnp.mean(v * v, axis=-1, keepdims=True) + EPSILON) * gain


def attention_kernel(dims, len_ref, x_ref, g1_ref, gq_ref, gkv_ref, g2_ref, cos_ref, sin_ref,
                     wdq_hbm, wdkv_hbm, wuq_hbm, wuk_hbm, wuv_hbm, wout_hbm, ckv_hbm, kpe_hbm,
                     r_ref, u_ref, cnew_ref, knew_ref,
                     ql_s, qr_s, cn_s, kn_s, o_s, tr_s,
                     wdq, wdkv, wuq, wuk, wuv, wout, ckv_b, kpe_b, wsem, csem):
    heads, nope, rope, qk, lat, per, slots = dims
    rows = x_ref.shape[0]
    seq = ckv_hbm.shape[1]
    half = rope // 2
    steps = rows // per
    scale = MSCALE * MSCALE / math.sqrt(qk)

    def wcopy(src, dst, i):
        return pltpu.make_async_copy(src, dst, wsem.at[i])

    def ccopy(step, slot):
        at = pl.ds(step * per, per)
        return (pltpu.make_async_copy(ckv_hbm.at[at], ckv_b.at[slot], csem.at[slot, 0]),
                pltpu.make_async_copy(kpe_hbm.at[at], kpe_b.at[slot], csem.at[slot, 1]))

    c_dq = wcopy(wdq_hbm, wdq, 0)
    c_dkv = wcopy(wdkv_hbm, wdkv, 1)
    c_uk = wcopy(wuk_hbm, wuk, 2)
    c_uq = wcopy(wuq_hbm, wuq, 3)
    c_uv = wcopy(wuv_hbm, wuv, 4)
    c_out = wcopy(wout_hbm, wout, 5)
    for c in (c_dq, c_dkv, c_uk, c_uq):
        c.start()
    for s in range(slots):
        for c in ccopy(s, s):
            c.start()
    c_uv.start()
    c_out.start()

    tr_s[...] = jnp.zeros_like(tr_s)
    cos_t, sin_t = cos_ref[...], sin_ref[...]
    tr_s[0:half, 0:rows] = cos_t
    tr_s[half:rope, 0:rows] = cos_t
    tr_s[rope:rope + half, 0:rows] = -sin_t
    tr_s[rope + half:2 * rope, 0:rows] = sin_t
    table = tr_s[...].T[0:rows]
    cos2, sin2 = table[:, 0:rope], pltpu.roll(table, 128 - rope, axis=1)[:, 0:rope]
    group = 256 // rope
    cos_g = jnp.concatenate([cos2] * group, axis=1)
    sin_g = jnp.concatenate([sin2] * group, axis=1)

    a = normed(x_ref[...].astype(F32), g1_ref[...]).astype(BF16)
    c_dq.wait()
    cq = normed(dot(a, wdq[...]), gq_ref[...]).astype(BF16)
    c_dkv.wait()
    cn = normed(dot_nt(a, wdkv[0:lat]), gkv_ref[...]).astype(BF16)
    cnew_ref[...] = cn
    cn_s[...] = cn.astype(F32)
    kp = dot_nt(a, wdkv[lat:lat + rope])
    ks = dot_nt(a, jnp.concatenate([wdkv[lat + half:lat + rope], wdkv[lat:lat + half]], axis=0))
    kn = (kp * cos2 + ks * sin2).astype(BF16).astype(F32)
    kn_s[...] = kn
    tr_s[...] = jnp.zeros_like(tr_s)
    tr_s[0:rows, 0:rope] = kn
    knew_ref[...] = tr_s[...].T[0:rope, 0:rows].astype(BF16)

    c_uk.wait()
    c_uq.wait()
    lane = lax.broadcasted_iota(jnp.int32, (rows, 2 * nope), 1)

    def project(g, carry):
        base = g * (group * qk)
        for quad in range(group // 4):
            wn = jnp.concatenate(
                [wuq[pl.ds(pl.multiple_of(base + (quad * 4 + j) * qk, 32), nope), :] for j in range(4)], axis=0)
            q4 = dot_nt(cq, wn)
            for pair in range(2):
                qp = q4[:, pair * 2 * nope:(pair + 1) * 2 * nope]
                both = jnp.concatenate([jnp.where(lane < nope, qp, 0.0), jnp.where(lane >= nope, qp, 0.0)], axis=0)
                first = g * group + quad * 4 + pair * 2
                wk = wuk[pl.ds(pl.multiple_of(first * nope, 128), 2 * nope), :]
                ql = dot(both.astype(BF16), wk)
                ql = ql.astype(BF16).astype(F32)
                for i in range(lat // 128):
                    ql_s[i, pl.ds(pl.multiple_of(first * rows, 128), 2 * rows), :] = ql[:, i * 128:(i + 1) * 128]
        lows = [wuq[pl.ds(pl.multiple_of(base + j * qk + nope, 16), half), :] for j in range(group)]
        highs = [wuq[pl.ds(pl.multiple_of(base + j * qk + nope + half, 16), half), :] for j in range(group)]
        wp = jnp.concatenate([w for j in range(group) for w in (lows[j], highs[j])], axis=0)
        ws = jnp.concatenate([w for j in range(group) for w in (highs[j], lows[j])], axis=0)
        qr = (dot_nt(cq, wp) * cos_g + dot_nt(cq, ws) * sin_g).astype(BF16).astype(F32)
        for j in range(group):
            part = qr[:, 128 * (j * rope // 128):128 * (j * rope // 128) + 128]
            shift = (128 - (j * rope) % 128) % 128
            if shift:
                part = pltpu.roll(part, shift, axis=1)
            qr_s[pl.ds(pl.multiple_of((g * group + j) * rows, 64), rows), :] = part
        return carry

    lax.fori_loop(0, heads // group, project, 0)

    position = lax.broadcasted_iota(jnp.int32, (heads, seq), 1)

    def attend(step, carry):
        slot = lax.rem(step, slots)
        for c in ccopy(step, slot):
            c.wait()
        for j in range(per):
            b = step * per + j
            ql = jnp.concatenate([ql_s[i, pl.ds(b, heads, stride=rows), :] for i in range(lat // 128)], axis=1)
            qr = qr_s[pl.ds(b, heads, stride=rows), :][:, 0:rope]
            ck = ckv_b[slot, j]
            s = (dot_nt(ql.astype(BF16), ck) + dot(qr.astype(BF16), kpe_b[slot, j])) * scale
            s = jnp.where(position < len_ref[b], s, -jnp.inf)
            cn_b = cn_s[pl.ds(b, 1), :]
            kn_b = kn_s[pl.ds(b, 1), :]
            s_new = (jnp.sum(ql * cn_b, axis=1, keepdims=True) + jnp.sum(qr * kn_b, axis=1, keepdims=True)) * scale
            m = jnp.maximum(jnp.max(s, axis=1, keepdims=True), s_new)
            e = jnp.exp(s - m)
            e_new = jnp.exp(s_new - m)
            total = jnp.sum(e, axis=1, keepdims=True) + e_new
            acc = dot(e.astype(BF16), ck) + e_new.astype(BF16).astype(F32) * cn_b
            out = (acc / total).astype(BF16).astype(F32)
            for i in range(lat // 128):
                ql_s[i, pl.ds(b, heads, stride=rows), :] = out[:, i * 128:(i + 1) * 128]

        @pl.when(step + slots < steps)
        def _():
            for c in ccopy(step + slots, slot):
                c.start()

        return carry

    lax.fori_loop(0, steps, attend, 0)

    c_uv.wait()
    quad_lane = lax.broadcasted_iota(jnp.int32, (rows, 4 * nope), 1) // nope

    def head_out(g, carry):
        at = pl.ds(pl.multiple_of(g * 4 * rows, 256), 4 * rows)
        lat_out = jnp.concatenate([ql_s[i, at, :] for i in range(lat // 128)], axis=1).astype(BF16)
        full = dot_nt(lat_out, wuv[pl.ds(pl.multiple_of(g * 4 * nope, 256), 4 * nope), :])
        o = full[0:rows]
        for j in range(1, 4):
            o = jnp.where(quad_lane == j, full[j * rows:(j + 1) * rows], o)
        o_s[g] = o.astype(BF16)
        return carry

    lax.fori_loop(0, heads // 4, head_out, 0)

    c_out.wait()
    o_all = jnp.concatenate([o_s[g] for g in range(heads // 4)], axis=1)
    width = 512
    sq = jnp.zeros((rows, 1), F32)
    for n in range(wout.shape[1] // width):
        at = slice(n * width, (n + 1) * width)
        res = (x_ref[:, at].astype(F32) + dot(o_all, wout[:, at])).astype(BF16)
        r_ref[:, at] = res
    u_ref[...] = normed(r_ref[...].astype(F32), g2_ref[...]).astype(BF16)


def attention_rows(hidden, ckv_cache, kpe_cache, cache_len, rope_cos, rope_sin, norm_attn, w_dq, norm_q, w_uq, w_dkv, norm_kv, w_uk, w_uv, w_out, norm_mlp):
    rows, width = hidden.shape
    q_lora, heads, qk = w_uq.shape
    lat, _, nope = w_uk.shape
    rope = kpe_cache.shape[2]
    seq = ckv_cache.shape[1]
    per, slots = 4, 3
    dims = (heads, nope, rope, qk, lat, per, slots)
    vm = pl.BlockSpec(memory_space=pltpu.VMEM)
    hbm = pl.BlockSpec(memory_space=pl.ANY)
    wdkv_t = w_dkv.T
    wuq_t = w_uq.transpose(1, 2, 0).reshape(heads * qk, q_lora)
    wuk_t = w_uk.transpose(1, 2, 0).reshape(heads * nope, lat)
    wuv_t = w_uv.transpose(1, 2, 0).reshape(heads * nope, lat)
    wout2 = w_out.reshape(heads * nope, width)
    r, u, cn, kn_t = pl.pallas_call(
        functools.partial(attention_kernel, dims),
        out_shape=(jax.ShapeDtypeStruct((rows, width), BF16), jax.ShapeDtypeStruct((rows, width), BF16),
                   jax.ShapeDtypeStruct((rows, lat), BF16), jax.ShapeDtypeStruct((rope, rows), BF16)),
        in_specs=[pl.BlockSpec(memory_space=pltpu.SMEM)] + [vm] * 7 + [hbm] * 8,
        out_specs=(vm,) * 4,
        scratch_shapes=[
            pltpu.VMEM((lat // 128, heads * rows, 128), F32),
            pltpu.VMEM((heads * rows, 128), F32),
            pltpu.VMEM((rows, lat), F32),
            pltpu.VMEM((rows, rope), F32),
            pltpu.VMEM((heads // 4, rows, 4 * nope), BF16),
            pltpu.VMEM((128, 128), F32),
            pltpu.VMEM(w_dq.shape, BF16),
            pltpu.VMEM(wdkv_t.shape, BF16),
            pltpu.VMEM(wuq_t.shape, BF16),
            pltpu.VMEM(wuk_t.shape, BF16),
            pltpu.VMEM(wuv_t.shape, BF16),
            pltpu.VMEM(wout2.shape, BF16),
            pltpu.VMEM((slots, per, seq, lat), BF16),
            pltpu.VMEM((slots, per, rope, seq), BF16),
            pltpu.SemaphoreType.DMA((6,)),
            pltpu.SemaphoreType.DMA((slots, 2)),
        ],
        compiler_params=pltpu.CompilerParams(vmem_limit_bytes=VMEM_LIMIT),
        name="attention",
    )(cache_len, hidden, norm_attn.reshape(1, -1), norm_q.reshape(1, -1), norm_kv.reshape(1, -1), norm_mlp.reshape(1, -1),
      rope_cos.T, rope_sin.T, w_dq, wdkv_t, wuq_t, wuk_t, wuv_t, wout2, ckv_cache, kpe_cache.transpose(0, 2, 1))
    return r, u, cn, kn_t.T


def solution(mesh):
    row_spec = P(('rep', 'dp'), None)
    cube_spec = P(('rep', 'dp'), None, None)
    full_spec = P()
    in_specs = (row_spec, cube_spec, cube_spec, P(('rep', 'dp')), row_spec, row_spec,
                full_spec, full_spec, full_spec, full_spec, full_spec, full_spec, full_spec, full_spec, full_spec, full_spec,
                P(None, 'dp'), P(None, 'dp'), P('dp', None))

    def local_step(hidden, ckv_cache, kpe_cache, cache_len, rope_cos, rope_sin, norm_attn, w_dq, norm_q, w_uq, w_dkv, norm_kv, w_uk, w_uv, w_out, norm_mlp, w_gate, w_up, w_down):
        residual, mlp_in, ckv_new, kpe_new = attention_rows(
            hidden, ckv_cache, kpe_cache, cache_len, rope_cos, rope_sin, norm_attn, w_dq, norm_q, w_uq, w_dkv, norm_kv, w_uk, w_uv, w_out, norm_mlp)
        group_in = lax.all_gather(mlp_in, 'dp', axis=0, tiled=True)
        gate_val = jnp.dot(group_in, w_gate, preferred_element_type=jnp.float32)
        up_val = jnp.dot(group_in, w_up, preferred_element_type=jnp.float32)
        act_val = (jax.nn.silu(gate_val) * up_val).astype(jnp.bfloat16)
        partial_sum = jnp.dot(act_val, w_down, preferred_element_type=jnp.float32)
        mlp_rows = lax.psum_scatter(partial_sum, 'dp', scatter_dimension=0, tiled=True)
        out_hidden = (residual.astype(jnp.float32) + mlp_rows).astype(jnp.bfloat16)
        return out_hidden, ckv_new, kpe_new

    return jax.shard_map(local_step, mesh=mesh, in_specs=in_specs, out_specs=(row_spec, row_spec, row_spec), check_vma=False)
```

time: 178 us -> 156 us (0.88)
  matrix products: 84.2 us -> 18 us
  Pallas kernels: 0 us -> 55.8 us
  other arithmetic: 15.2 us -> 1.87 us
    dot_general x10 -> x0, matrix products: 65.7 us -> none  [the longest x1 20.4 us: attention_rows(): jnp.einsum('bhl,btl->bht', q_abs, ckv_cache, preferred_element_type=jnp.f...]
    pallas_call x0 -> x1, Pallas kernels: none -> 55.8 us  [attention_rows(): pl.pallas_call(functools.partial(attention_kernel, dims), out_shape=(jax....]
    reduce_sum x3 -> x0, other arithmetic: 9.82 us -> none  [the longest x1 8.47 us: attention_rows(): norm_sum = jnp.sum(exp_cache, axis=-1) + exp_new]
    reshape x0 -> x3, local copies, waits for them, and re-layouts: none -> 3.91 us  [the longest x1 1.32 us: attention_rows(): norm_attn.reshape(1, -1)]
    unnamed x26 -> x4, local copies, waits for them, and re-layouts: 1.88 us -> 0.01 us
where the time goes in v1:
time: 156 us; the launch traced here: 155 us
  waiting for transfers between devices  61.7 us (40%)
  Pallas kernels  55.8 us (36%)
  matrix products  18 us (12%)
  between operations  14.1 us (9%)
  local copies, waits for them, and re-layouts  3.92 us (3%)
  other arithmetic  1.87 us (1%)
    pallas_call x1, Pallas kernels, attention_rows(): pl.pallas_call(functools.partial(attention_kernel, dims), out_shape=(jax....  55.8 us
    reduce_scatter x1, waiting for transfers between devices, local_step(): lax.psum_scatter(partial_sum, 'dp', scatter_dimension=0, tiled=True)  36.6 us
    all_gather x1, waiting for transfers between devices, local_step(): group_in = lax.all_gather(mlp_in, 'dp', axis=0, tiled=True)  24.9 us
    dot_general x1, matrix products, local_step(): partial_sum = jnp.dot(act_val, w_down, preferred_element_type=jnp.float32)  11.3 us
    dot_general x1, matrix products, local_step(): gate_val = jnp.dot(group_in, w_gate, preferred_element_type=jnp.float32)  6.62 us
  transfers between devices with their start and end apart: 2, of which 2 were waited for; matrix products, arithmetic and copies ran while one was open for 0% of the time, Pallas kernels for 0%

profile of v1, /device:TPU:112, one launch (start us, length us, event | category | flops | bytes accessed | tf_op | source)
XLA Modules:
  0.0 155.4 jit_solution(2751886072315705299)
XLA Ops:
  7.2 0.1 all-gather.2.cloned.1.call-start
  7.2 1.3 reshape.31.gq_ref
  8.5 1.3 reshape.30.g1_ref
  9.8 1.3 reshape.33.g2_ref
  11.2 55.8 %attention.1 = (bf16[64,2560]{1,0:T(8,128)(2,1)}, bf16[64,2560]{1,0:T(8,128)(2,1)}, bf16[64,256]{1,0:T(8,128)(2,1)}, bf16[32,64]{1,0:T(8,128)(2,1)}) custom-call(s32[64]{0:T(128)} %len_ref.1, bf16[64,2560]{1,0:T(8,128)(2,1)} %x_ref.1, f32[1,2560]{1,0:T(1,128)} %reshape.30.g1_ref, f32[1,768]{1,0:T(1,128)} %reshape.31.gq_ref, f32[1,256]{1,0:T(1,128)} %bitcast.29, ...), custom_call_target="tpu_custom_call" | custom-call | tf_op jit(solution)/shard_map/attention/pallas_call | solution.py:201
  67.0 0.1 all-gather.2.cloned.1.call-update
  67.0 0.1 reduce-scatter.2.cloned.1.call-start
  67.1 24.9 %all-gather.2.cloned.1.call-done = bf16[512,2560]{1,0:T(8,128)(2,1)} async-done(((bf16[64,2560]{1,0:T(8,128)(2,1)}), bf16[512,2560]{1,0:T(8,128)(2,1)}) %all-gather.2.cloned.1.call-update) | async-done | bytes 2621456 | tf_op jit(solution)/shard_map/all_gather | solution.py:243
  92.0 0.0 copy-start.1
  92.1 6.6 %fusion.2 = f32[512,800]{0,1:T(8,128)} fusion(bf16[512,2560]{1,0:T(8,128)(2,1)} %all-gather.2.cloned.1.call-done, bf16[2560,800]{0,1:T(8,128)(2,1)} %param.35), kind=kOutput, calls=%fused_computation.4 | convolution fusion | flops 2097152000 | bytes 8355840 | tf_op jit(solution)/shard_map/dot_general | solution.py:244
  98.7 0.0 copy-done.1
  98.7 11.3 %fusion = f32[512,2560]{1,0:T(8,128)} fusion(bf16[800,2560]{1,0:T(8,128)(2,1)} %param.37, f32[512,800]{0,1:T(8,128)} %fusion.2, bf16[512,2560]{1,0:T(8,128)(2,1)S(1)} %copy-done.1, bf16[2560,800]{0,1:T(8,128)(2,1)} %param.36), kind=kOutput, calls=%fused_computation.2 | convolution fusion | flops 4196761600 | bytes 17694720 | tf_op jit(solution)/shard_map/dot_general | solution.py:247
  110.0 0.0 copy-start
  110.0 0.1 reduce-scatter.2.cloned.1.call-update
  110.1 36.6 %reduce-scatter.2.cloned.1.call-done = f32[64,2560]{1,0:T(8,128)} async-done(((f32[512,2560]{1,0:T(8,128)}), f32[64,2560]{1,0:T(8,128)}) %reduce-scatter.2.cloned.1.call-update) | async-done | bytes 655376 | tf_op jit(solution)/shard_map/reduce_scatter | solution.py:248
  146.7 0.0 copy-done
  146.7 1.9 %add_convert_fusion = bf16[64,2560]{1,0:T(8,128)(2,1)} fusion(f32[64,2560]{1,0:T(8,128)} %reduce-scatter.2.cloned.1.call-done, bf16[64,2560]{1,0:T(8,128)(2,1)S(1)} %copy-done), kind=kLoop, calls=%fused_computation.1 | loop fusion | flops 491520 | bytes 1310720 | tf_op jit(solution)/shard_map/convert_element_type | solution.py:249
Async XLA Ops:
  7.2 84.9 %all-gather.2.cloned.1.call-start = ((), (), s32[]{:S(2)}) async-start(), calls=%async_computation.1 | async-start | bytes 2949120 | tf_op jit(solution)/shard_map/all_gather | solution.py:243
  67.0 79.6 %reduce-scatter.2.cloned.1.call-start = ((), (), s32[]{:S(2)}) async-start(), calls=%async_computation.2 | async-start | bytes 5898240 | tf_op jit(solution)/shard_map/reduce_scatter | solution.py:248
  92.0 6.6 %copy-start.1 = (bf16[512,2560]{1,0:T(8,128)(2,1)S(1)}, bf16[512,2560]{1,0:T(8,128)(2,1)}, u32[]{:S(2)}) copy-start(bf16[512,2560]{1,0:T(8,128)(2,1)} %all-gather.2.cloned.1.call-done) | copy-start | bytes 7864324
  110.0 36.7 %copy-start = (bf16[64,2560]{1,0:T(8,128)(2,1)S(1)}, bf16[64,2560]{1,0:T(8,128)(2,1)}, u32[]{:S(2)}) copy-start(bf16[64,2560]{1,0:T(8,128)(2,1)} %get-tuple-element.7) | copy-start | bytes 983044
Sparse Core Ops, SparseCore 0:
  67.2 24.8 all-gather.1
  110.2 36.4 reduce-scatter.1
